TPU v7x, 32 devices: a whole 2x2x4 slice. The times are simulated.
32 devices in a mesh: dp: 16 (over z, y, x), mp: 2 (over core).
Axes of the slice: x: 2, y: 2, z: 4, core: 2. Of those that a mesh axis runs over, the one named last changes fastest.
Arguments:
- patches: bfloat16 [8192, 3200], P(('dp', 'mp')), may hold values from -120 to 120
- ln_gain: bfloat16 [3200], replicated, may hold values from 0.099609375 to 1.8984375
- ln_bias: bfloat16 [3200], replicated, may hold values from -3 to 3
- w_proj: bfloat16 [3200, 4096], P(None, 'mp'), may hold values from -0.109375 to 0.109375
- proj_bias: bfloat16 [4096], P('mp'), may hold values from -3 to 3
- rms_gain: bfloat16 [4096], replicated, may hold values from 0.099609375 to 1.8984375
- w_qkv: bfloat16 [4096, 3072], P(None, 'mp'), may hold values from -4 to 4
- image_counts: int32 [64, 8], replicated, may hold values from 1 to 16, as said below
- source_shift: int32 [32], replicated, may hold values from 0 to 15, as said below
Outputs:
- attended: bfloat16 [8192, 2048], P('dp', 'mp')
Inputs may be any that keep to these rules, and one draw needn't show every extreme that they name: `image_counts`: row g holds the counts of the 8 images of tile g. In every draw all images of the tiles of some dp index hold 16 tokens. No value stands more than 2 times in source_shift, and some value stands exactly 2 times.
All inputs are finite; a program needn't handle non-finite values.
Results may differ from a plain program's by a relative error of at most 0.012.
Values may be sent and summed in bfloat16 or wider, within the bound.
A program may use at most 128 MiB of HBM per device.

v0:
```python
import functools

import jax
import jax.numpy as jnp
import numpy as np
from jax import lax
from jax.experimental import pallas as pl
from jax.experimental.pallas import tpu as pltpu
from jax.sharding import PartitionSpec as P

HEAD_SIZE = 128
TILE = 128
QUERY_PER_KEY = 4
COL_TILE = 256
CHUNKS = (256, 256)

norm_epsilon = 1e-05
rms_epsilon = 1e-05
rotary_base = 500000.0

F32 = jnp.float32
BF16 = jnp.bfloat16
MESH = pl.DeviceIdType.MESH


def shift_order(senders):
    return sorted(range(senders), key=lambda v: (abs(v - senders // 2), v))


def rotary_parts():
    frequency = np.float32(rotary_base) ** (
        -(np.arange(HEAD_SIZE // 2, dtype=np.float32) * np.float32(2.0 / HEAD_SIZE))
    )
    angles = np.arange(TILE, dtype=np.float32)[:, None] * frequency[None, :].astype(np.float32)
    cos = np.cos(angles.astype(np.float64)).astype(np.float32)
    sin = np.sin(angles.astype(np.float64)).astype(np.float32)
    parts = []
    for table in (np.concatenate([cos, cos], 1), np.concatenate([-sin, sin], 1)):
        rest = table
        for _ in range(3):
            term = rest.astype(jnp.bfloat16)
            parts.append(term)
            rest = rest - term.astype(np.float32)
    return np.concatenate(parts, axis=1)


def chunk_list(box_rows):
    sizes = list(CHUNKS)
    while sum(sizes) < box_rows:
        sizes.append(CHUNKS[-1])
    return sizes


def gelu(v):
    return 0.5 * v * (1.0 + lax.erf(v * np.float32(0.5**0.5)))


def iota(shape, axis):
    return lax.broadcasted_iota(jnp.int32, shape, axis)


def lane_sum(x):
    return jnp.sum(x, axis=1, keepdims=True)


def kernel(
    senders,
    order,
    ln_gain,
    ln_bias,
    proj_bias,
    rms_gain,
    counts,
    source_shift,
    table,
    patches,
    w_proj,
    w_qkv,
    out,
    raw,
    w1,
    w2,
    normed,
    picked,
    hidden,
    rms_normed,
    pre,
    bias,
    proj,
    outbox,
    inbox,
    placed,
    raw_sem,
    out_sem,
    w1_sem,
    w2_sem,
    norm_send,
    norm_recv,
    hid_send,
    hid_recv,
    a2a_send,
    a2a_recv,
):
    me = lax.axis_index("dp")
    core = lax.axis_index("mp")
    peer = 1 - core
    half, d_vit = raw.shape
    rows = 2 * half
    box_rows = outbox.shape[0]
    block = box_rows // senders
    images = source_shift.shape[0]
    tiles_dev = rows // TILE
    img_tile = images // tiles_dev
    img_most = TILE // img_tile
    pair_slots = block // img_most
    sizes = chunk_list(box_rows)
    chunks = len(sizes)
    firsts = [sum(sizes[:c]) for c in range(chunks)]
    half_cols = w_proj.shape[1]
    qkv_cols = w_qkv.shape[1]
    groups = qkv_cols // ((QUERY_PER_KEY + 2) * HEAD_SIZE)
    tiles1 = half_cols // COL_TILE
    tiles2 = qkv_cols // COL_TILE

    part = half // 2

    def raw_copy(i):
        at = pl.ds(i * part, part)
        return pltpu.make_async_copy(patches.at[at], raw.at[at], raw_sem.at[i])

    for i in range(2):
        raw_copy(i).start()

    barrier = pltpu.get_barrier_semaphore()
    pl.semaphore_signal(barrier, inc=1, device_id={"mp": peer}, device_id_type=MESH)
    for v in range(1, senders):
        pl.semaphore_signal(
            barrier, inc=1, device_id={"dp": lax.rem(me + v, senders)}, device_id_type=MESH
        )

    def w1_copy(j):
        cols = pl.ds(pl.multiple_of(j * COL_TILE, COL_TILE), COL_TILE)
        return pltpu.make_async_copy(w_proj.at[:, cols], w1.at[:, cols], w1_sem.at[j])

    def w2_copy(j):
        cols = pl.ds(pl.multiple_of(j * COL_TILE, COL_TILE), COL_TILE)
        return pltpu.make_async_copy(w_qkv.at[:, cols], w2.at[:, cols], w2_sem.at[j])

    gain_f = ln_gain[...].reshape(1, -1).astype(F32)
    bias_f = ln_bias[...].reshape(1, -1).astype(F32)

    def norm_copy(i):
        mine = normed.at[pl.ds(pl.multiple_of(core * half + i * part, part), part)]
        return pltpu.make_async_remote_copy(
            src_ref=mine,
            dst_ref=mine,
            send_sem=norm_send.at[i],
            recv_sem=norm_recv.at[i],
            device_id={"mp": peer},
            device_id_type=MESH,
        )

    for i in range(2):
        raw_copy(i).wait()
        if i == 0:
            for j in range(tiles1):
                w1_copy(j).start()
            for j in range(tiles2):
                w2_copy(j).start()

        @pl.loop(0, part // 16, unroll=2)
        def _(r):
            values = raw[pl.ds(pl.multiple_of(i * part + r * 16, 16), 16), :].astype(F32)
            centred = values - jnp.mean(values, axis=-1, keepdims=True)
            variance = jnp.mean(centred * centred, axis=-1, keepdims=True)
            scaled = centred * lax.rsqrt(variance + norm_epsilon) * gain_f + bias_f
            to = pl.ds(pl.multiple_of(core * half + i * part + r * 16, 16), 16)
            normed[to, :] = scaled.astype(BF16)

        if i == 0:
            pl.semaphore_wait(barrier, senders)
        norm_copy(i).start()

    sq = (images, images)
    k_at, l_at = iota(sq, 0), iota(sq, 1)
    eye = k_at == l_at
    before = l_at < k_at
    same_tile = (k_at // img_tile) == (l_at // img_tile)

    def to_row(col):
        return jnp.sum(jnp.where(eye, col, 0), axis=0, keepdims=True)

    tiles_all = counts.shape[1]
    spread = (iota((img_tile, images), 1) % img_tile == iota((img_tile, images), 0)).astype(F32)
    wide = lax.dot_general(
        counts[...].astype(F32).astype(BF16),
        spread.astype(BF16),
        (((0,), (0,)), ((), ())),
        preferred_element_type=F32,
    )
    own_tile = iota((tiles_all, images), 1) // img_tile == iota((tiles_all, images), 0) % tiles_dev
    wide = jnp.where(own_tile, wide, 0.0).astype(BF16)
    gather = (iota((senders, tiles_all), 1) // tiles_dev == iota((senders, tiles_all), 0)).astype(F32)
    per_dest = jnp.dot(gather.astype(BF16), wide, preferred_element_type=F32).astype(jnp.int32)

    shift_row = source_shift[...].reshape(1, images)
    shift = lane_sum(jnp.where(eye, shift_row, 0))
    dest = me - shift
    dest = jnp.where(dest < 0, dest + senders, dest)
    counts_to = jnp.zeros(sq, jnp.int32)
    place = jnp.zeros((images, 1), jnp.int32)
    for v in range(senders):
        counts_to = jnp.where(dest == v, per_dest[v : v + 1, :], counts_to)
        place = jnp.where(shift == order[v], v, place)
    sent_row = jnp.sum(jnp.where(eye, counts_to, 0), axis=0, keepdims=True)
    starts = lane_sum(jnp.where(before, sent_row, 0))
    far_offset = lane_sum(jnp.where(before & same_tile, counts_to, 0))
    rank = lane_sum(jnp.where(before & (shift_row == shift), 1, 0))
    slot_row = to_row(place * pair_slots + rank)
    starts_row = to_row(starts)
    far_row = to_row(far_offset)

    dest_at = iota(per_dest.shape, 0)
    my_row = jnp.sum(jnp.where(dest_at == me, per_dest, 0), axis=0, keepdims=True)
    my_offset = lane_sum(jnp.where(before & same_tile, my_row, 0))
    my_off_row = to_row(my_offset)

    def of_chunk(c):
        row_at = iota((sizes[c], images), 0) + firsts[c]
        hit = slot_row == row_at // img_most
        inside = iota((sizes[c], 1), 0) % img_most
        src = lane_sum(jnp.where(hit, starts_row, 0)) + inside
        pos = lane_sum(jnp.where(hit, far_row, 0)) + inside
        return src, pos

    def copy_hidden(c, part):
        ref = hidden.at[
            core, pl.ds(firsts[c], sizes[c]), pl.ds(part * half_cols // 2, half_cols // 2)
        ]
        return pltpu.make_async_remote_copy(
            src_ref=ref,
            dst_ref=ref,
            send_sem=hid_send.at[2 * c + part],
            recv_sem=hid_recv.at[2 * c + part],
            device_id={"mp": peer},
            device_id_type=MESH,
        )

    def copy_block(o):
        at = pl.ds(o * block, block)
        return pltpu.make_async_remote_copy(
            src_ref=outbox.at[at],
            dst_ref=inbox.at[at],
            send_sem=a2a_send.at[o],
            recv_sem=a2a_recv.at[o],
            device_id={"dp": lax.rem(me + senders - order[o], senders)},
            device_id_type=MESH,
        )

    pick_tile = 128 * max(w for w in range(1, 9) if (d_vit // 128) % w == 0)
    chunk_rows = [of_chunk(c) for c in range(chunks)]
    for i in range(2):
        norm_copy(i).wait_recv()

    def project(c):
        size = sizes[c]
        rows_at = pl.ds(firsts[c], size)
        select = jnp.where(iota((size, rows), 1) == chunk_rows[c][0], 1.0, 0.0).astype(BF16)

        @pl.loop(0, d_vit // pick_tile)
        def _(j):
            cols = pl.ds(pl.multiple_of(j * pick_tile, pick_tile), pick_tile)
            picked[:size, cols] = jnp.dot(
                select, normed[:, cols], preferred_element_type=F32
            ).astype(BF16)

        def columns(j):
            return pl.ds(pl.multiple_of(j * COL_TILE, COL_TILE), COL_TILE)

        def multiply(j, slot):
            if c == 0:
                w1_copy(j).wait()
            pre[slot, :size] = jnp.dot(
                picked[:size], w1[:, columns(j)], preferred_element_type=F32
            )

        bias_row = proj_bias[...].reshape(1, -1)

        def activate(j, slot):
            x = pre[slot, :size] + bias[:, columns(j)]
            hidden[core, rows_at, columns(j)] = gelu(x).astype(BF16)

        if c == 0:
            bias[...] = bias_row.astype(F32)
        multiply(0, 0)
        pairs = tiles1 // 2
        for part in range(2):
            low, high = part * pairs // 2, (part + 1) * pairs // 2 - part

            @pl.loop(low, high)
            def _(i):
                multiply(2 * i + 1, 1)
                activate(2 * i, 0)
                multiply(2 * i + 2, 0)
                activate(2 * i + 1, 1)

            if part == 1:
                multiply(tiles1 - 1, 1)
                activate(tiles1 - 2, 0)
                activate(tiles1 - 1, 1)
            copy_hidden(c, part).start()

    q_at = iota((QUERY_PER_KEY * TILE, TILE), 0) % TILE
    s_at = iota((QUERY_PER_KEY * TILE, TILE), 1)
    allowed = (q_at // img_most == s_at // img_most) & (s_at <= q_at)

    def finish(c):
        size = sizes[c]
        for part in range(2):
            copy_hidden(c, part).wait_recv()
        pos_hot = jnp.where(iota((size, TILE), 1) == chunk_rows[c][1], 1.0, 0.0).astype(BF16)
        terms = jnp.dot(pos_hot, table[...], preferred_element_type=F32)
        w = HEAD_SIZE
        cos = terms[:, :w] + terms[:, w : 2 * w] + terms[:, 2 * w : 3 * w]
        sin = terms[:, 3 * w : 4 * w] + terms[:, 4 * w : 5 * w] + terms[:, 5 * w :]

        gains = rms_gain[...].reshape(1, -1).astype(F32)

        @pl.loop(0, size // 16, unroll=2)
        def _(r):
            at = pl.ds(pl.multiple_of(firsts[c] + r * 16, 16), 16)
            to = pl.ds(pl.multiple_of(r * 16, 16), 16)
            total = jnp.zeros((16, 1), F32)
            for h in range(2):
                x = hidden[h, at, :].astype(F32)
                total = total + jnp.sum(x * x, axis=-1, keepdims=True)
            scale = lax.rsqrt(total * (1.0 / (2 * half_cols)) + rms_epsilon)
            for h in range(2):
                x = hidden[h, at, :].astype(F32)
                g = gains[:, h * half_cols : (h + 1) * half_cols]
                rms_normed[to, h * half_cols : (h + 1) * half_cols] = (x * scale * g).astype(BF16)

        @pl.loop(0, tiles2)
        def _(j):
            if c == 0:
                w2_copy(j).wait()
            cols = pl.ds(pl.multiple_of(j * COL_TILE, COL_TILE), COL_TILE)
            proj[:size, cols] = jnp.dot(rms_normed[:size], w2[:, cols], preferred_element_type=F32)

        def head(first, h, rotate):
            v = proj[first : first + TILE, h * w : (h + 1) * w]
            if rotate:
                v = v * cos[first : first + TILE] + pltpu.roll(v, w // 2, 1) * sin[first : first + TILE]
            return v.astype(BF16)

        for first in range(0, size, TILE):
            for g in range(groups):
                h0 = g * (QUERY_PER_KEY + 2)
                q = jnp.concatenate(
                    [head(first, h0 + i, True) for i in range(QUERY_PER_KEY)], axis=0
                )
                k = head(first, h0 + QUERY_PER_KEY, True)
                v = head(first, h0 + QUERY_PER_KEY + 1, False)
                scores = lax.dot_general(
                    q, k, (((1,), (1,)), ((), ())), preferred_element_type=F32
                ) * np.float32(HEAD_SIZE ** (-0.5))
                scores = jnp.where(allowed, scores, -1e30)
                weights = jnp.exp(scores - jnp.max(scores, axis=-1, keepdims=True))
                probs = (weights / jnp.sum(weights, axis=-1, keepdims=True)).astype(BF16)
                got = jnp.dot(probs, v, preferred_element_type=F32).astype(BF16)
                for i in range(QUERY_PER_KEY):
                    a = (g * QUERY_PER_KEY + i) * w
                    outbox[firsts[c] + first : firsts[c] + first + TILE, a : a + w] = got[
                        i * TILE : (i + 1) * TILE
                    ]
        for o in range(firsts[c] // block, (firsts[c] + size) // block):
            if o < senders - 1:
                copy_block(o).start()
        if c == chunks - 1:
            inbox[box_rows - block :, :] = outbox[box_rows - block :, :]

    for c in range(chunks):
        project(c)
        finish(c)

    t_at = iota((TILE, images), 0)
    image_at = iota((TILE, images), 1)
    place_of = []
    for t in range(tiles_dev):
        hit = (image_at // img_tile == t) & (t_at >= my_off_row) & (t_at < my_off_row + my_row)
        at = jnp.where(hit, slot_row * img_most + (t_at - my_off_row) + 1, 0)
        place_of.append(lane_sum(at) - 1)

    def out_copy(t):
        at = pl.ds(t * TILE, TILE)
        return pltpu.make_async_copy(placed.at[at], out.at[at], out_sem.at[t])

    for o in range(senders - 1):
        copy_block(o).wait_recv()
    for t in range(tiles_dev):
        select = jnp.where(iota((TILE, box_rows), 1) == place_of[t], 1.0, 0.0).astype(BF16)
        placed[t * TILE : (t + 1) * TILE, :] = jnp.dot(
            select, inbox[...], preferred_element_type=F32
        ).astype(BF16)
        out_copy(t).start()
    for t in range(tiles_dev):
        out_copy(t).wait()

    for i in range(2):
        norm_copy(i).wait_send()
    for c in range(chunks):
        for part in range(2):
            copy_hidden(c, part).wait_send()
    for o in range(senders - 1):
        copy_block(o).wait_send()


def local(
    patches, ln_gain, ln_bias, w_proj, proj_bias, rms_gain, w_qkv, image_counts, source_shift
):
    senders = lax.axis_size("dp")
    order = shift_order(senders)
    half, d_vit = patches.shape
    rows = 2 * half
    half_cols = w_proj.shape[1]
    qkv_cols = w_qkv.shape[1]
    groups = qkv_cols // ((QUERY_PER_KEY + 2) * HEAD_SIZE)
    out_cols = groups * QUERY_PER_KEY * HEAD_SIZE
    images = source_shift.shape[0]
    img_most = TILE // (images // (rows // TILE))
    pair_slots = (images + senders - 1) // senders
    box_rows = senders * pair_slots * img_most
    sizes = chunk_list(box_rows)
    chunks = len(sizes)
    size = max(sizes)
    vmem = pl.BlockSpec(memory_space=pltpu.VMEM)
    hbm = pl.BlockSpec(memory_space=pl.ANY)
    dma = pltpu.SemaphoreType.DMA
    return pl.pallas_call(
        functools.partial(kernel, senders, order),
        out_shape=jax.ShapeDtypeStruct((rows, out_cols), BF16),
        in_specs=[vmem] * 7 + [hbm] * 3,
        out_specs=hbm,
        scratch_shapes=[
            pltpu.VMEM((half, d_vit), BF16),
            pltpu.VMEM(w_proj.shape, BF16),
            pltpu.VMEM(w_qkv.shape, BF16),
            pltpu.VMEM((rows, d_vit), BF16),
            pltpu.VMEM((size, d_vit), BF16),
            pltpu.VMEM((2, box_rows, half_cols), BF16),
            pltpu.VMEM((size, 2 * half_cols), BF16),
            pltpu.VMEM((2, size, COL_TILE), F32),
            pltpu.VMEM((1, half_cols), F32),
            pltpu.VMEM((size, qkv_cols), F32),
            pltpu.VMEM((box_rows, out_cols), BF16),
            pltpu.VMEM((box_rows, out_cols), BF16),
            pltpu.VMEM((rows, out_cols), BF16),
            dma((2,)),
            dma((rows // TILE,)),
            dma((half_cols // COL_TILE,)),
            dma((qkv_cols // COL_TILE,)),
            dma((2,)),
            dma((2,)),
            dma((2 * chunks,)),
            dma((2 * chunks,)),
            dma((senders,)),
            dma((senders,)),
        ],
        compiler_params=pltpu.CompilerParams(
            collective_id=0, has_side_effects=True, vmem_limit_bytes=60 * 1024 * 1024
        ),
        name="projector_attention",
    )(
        ln_gain,
        ln_bias,
        proj_bias,
        rms_gain,
        image_counts.T,
        source_shift,
        jnp.asarray(rotary_parts()),
        patches,
        w_proj,
        w_qkv,
    )


def solution(mesh):
    in_specs = (
        P(("dp", "mp"), None),
        P(),
        P(),
        P(None, "mp"),
        P("mp"),
        P(),
        P(None, "mp"),
        P(),
        P(),
    )
    out_specs = P("dp", "mp")
    return jax.shard_map(local, mesh=mesh, in_specs=in_specs, out_specs=out_specs, check_vma=False)
```

profile of v0, /device:TPU:0, one launch (start us, length us, event | category | flops | bytes accessed | tf_op | source)
XLA Modules:
  0.0 59.7 jit_solution(14662054428260556923)
XLA Ops:
  0.0 57.5 %projector_attention.1 = bf16[512,1024]{1,0:T(8,128)(2,1)} custom-call(bf16[3200]{0:T(1024)(128)(2,1)} %ln_gain.1, bf16[3200]{0:T(1024)(128)(2,1)} %ln_bias.1, bf16[2048]{0:T(1024)(128)(2,1)} %proj_bias.1, bf16[4096]{0:T(1024)(128)(2,1)} %rms_gain.1, s32[8,64]{1,0:T(8,128)} %bitcast.1, s32[32]{0:T(128)} %source_shift.1, ...), custom_call_target="tpu_custom_call" | custom-call | tf_op jit(solution)/shard_map/projector_attention/pallas_call | solution.py:439
  57.5 2.3 %copy.12 = bf16[512,1024]{1,0:T(8,128)(2,1)} copy(bf16[512,1024]{1,0:T(8,128)(2,1)} %projector_attention.1) | data formatting | bytes 2097152
where the time goes:
time: 59.9 us; the launch traced here: 59.7 us
  Pallas kernels  57.5 us (96%)
  local copies, waits for them, and re-layouts  2.26 us (4%)
    pallas_call x1, Pallas kernels, local(): pl.pallas_call(functools.partial(kernel, senders, order), out_shape=jax.S...  57.5 us
    unnamed x1, local copies, waits for them, and re-layouts  2.26 us

commit v1 on v0

v1 whole, which is shorter than its diff:
```python
import functools

import jax
import jax.numpy as jnp
import numpy as np
from jax import lax
from jax.experimental import pallas as pl
from jax.experimental.pallas import tpu as pltpu
from jax.sharding import PartitionSpec as P

HEAD_SIZE = 128
TILE = 128
QUERY_PER_KEY = 4
COL_TILE = 256
LANES = 128
PROJECT_ROWS = 512
CHUNK = 256

norm_epsilon = 1e-05
rms_epsilon = 1e-05
rotary_base = 500000.0

F32 = jnp.float32
BF16 = jnp.bfloat16
I32 = jnp.int32
MESH = pl.DeviceIdType.MESH


def shift_order(senders):
    return sorted(range(senders), key=lambda v: (abs(v - senders // 2), v))


def rotary_table(positions):
    frequency = np.float32(rotary_base) ** (
        -(np.arange(HEAD_SIZE // 2, dtype=np.float32) * np.float32(2.0 / HEAD_SIZE))
    )
    angles = np.arange(positions, dtype=np.float32)[:, None] * frequency[None, :].astype(np.float32)
    cos = np.cos(angles.astype(np.float64)).astype(np.float32)
    sin = np.sin(angles.astype(np.float64)).astype(np.float32)
    both = np.stack([np.concatenate([cos, cos], 1), np.concatenate([-sin, sin], 1)], axis=1)
    return both.reshape(2 * positions, HEAD_SIZE)


def gelu(v):
    return 0.5 * v * (1.0 + lax.erf(v * np.float32(0.5**0.5)))


def iota(shape, axis):
    return lax.broadcasted_iota(jnp.int32, shape, axis)


def lane_sum(x):
    return jnp.sum(x, axis=1, keepdims=True)


def row_sum(x):
    return jnp.sum(x, axis=0, keepdims=True)


def kernel(
    senders,
    order,
    ln_gain,
    ln_bias,
    proj_bias,
    rms_gain,
    counts,
    source_shift,
    table,
    patches,
    w_proj,
    w_qkv,
    inbox,
    meta_cols,
    meta_rows,
    raw,
    w1,
    w2,
    normed,
    spread,
    picked,
    hidden,
    squares,
    pre,
    bias,
    proj,
    cos_at,
    sin_at,
    outbox,
    cols_at,
    rows_at,
    plan,
    plan_at,
    raw_sem,
    w1_sem,
    w2_sem,
    plan_sem,
    meta_sem,
    own_sem,
    norm_send,
    norm_recv,
    hid_send,
    hid_recv,
    sq_send,
    sq_recv,
    a2a_send,
    a2a_recv,
):
    me = lax.axis_index("dp")
    core = lax.axis_index("mp")
    peer = 1 - core
    half, d_vit = raw.shape
    rows = 2 * half
    blocks = d_vit // LANES
    box_rows = outbox.shape[0]
    block = box_rows // senders
    images = source_shift.shape[0]
    tiles_dev = rows // TILE
    img_tile = images // tiles_dev
    img_most = TILE // img_tile
    slots = box_rows // img_most
    pair_slots = block // img_most
    half_cols = w_proj.shape[1]
    qkv_cols = w_qkv.shape[1]
    groups = qkv_cols // ((QUERY_PER_KEY + 2) * HEAD_SIZE)
    tiles1 = half_cols // COL_TILE
    pairs = tiles1 // 2
    tiles2 = qkv_cols // COL_TILE
    big = picked.shape[0]
    bigs = box_rows // big
    chunks = box_rows // CHUNK
    part = half // 2

    def raw_copy(i):
        at = pl.ds(i * part, part)
        return pltpu.make_async_copy(patches.at[at], raw.at[at], raw_sem.at[i])

    def w1_copy(j):
        cols = pl.ds(j * 2 * COL_TILE, 2 * COL_TILE)
        return pltpu.make_async_copy(w_proj.at[:, cols], w1.at[:, cols], w1_sem.at[j])

    def w2_copy(j):
        cols = pl.ds(j * 2 * COL_TILE, 2 * COL_TILE)
        return pltpu.make_async_copy(w_qkv.at[:, cols], w2.at[:, cols], w2_sem.at[j])

    for i in range(2):
        raw_copy(i).start()

    barrier = pltpu.get_barrier_semaphore()
    pl.semaphore_signal(barrier, inc=1, device_id={"mp": peer}, device_id_type=MESH)
    for v in range(1, senders):
        pl.semaphore_signal(
            barrier, inc=1, device_id={"dp": lax.rem(me + v, senders)}, device_id_type=MESH
        )

    sq = (images, images)
    k_at, l_at = iota(sq, 0), iota(sq, 1)
    eye = k_at == l_at
    before = l_at < k_at

    def to_row(col):
        return row_sum(jnp.where(eye, col, 0))

    def to_col(row):
        return lane_sum(jnp.where(eye, row, 0))

    tiles_all = counts.shape[1]
    image_counts = counts[...]
    earlier = jnp.zeros((img_tile, tiles_all), I32)
    for j in range(img_tile - 1):
        earlier += jnp.where(iota((img_tile, tiles_all), 0) > j, image_counts[j : j + 1, :], 0)
    counts_by = jnp.concatenate([image_counts] * tiles_dev, axis=0)
    earlier_by = jnp.concatenate([earlier] * tiles_dev, axis=0)
    tile_at = iota((images, tiles_all), 1)
    own_tile = iota((images, 1), 0) // img_tile

    shift_row = source_shift[...].reshape(1, images)
    shift = to_col(shift_row)
    dest = me - shift
    dest = jnp.where(dest < 0, dest + senders, dest)
    place = jnp.zeros((images, 1), I32)
    for v in range(senders):
        place = jnp.where(shift == order[v], v, place)
    there = tile_at == dest * tiles_dev + own_tile
    starts = lane_sum(jnp.where(before, to_row(lane_sum(jnp.where(there, counts_by, 0))), 0))
    far_offset = lane_sum(jnp.where(there, earlier_by, 0))
    rank = lane_sum(jnp.where(before & (shift_row == shift), 1, 0))
    slot = place * pair_slots + rank

    slot_hit = slot == iota((images, LANES), 1)
    plan[0:1, :] = row_sum(jnp.where(slot_hit, starts * blocks, 0))
    plan[1:2, :] = row_sum(jnp.where(slot_hit, far_offset * 2, 0))
    plan_copy = pltpu.make_async_copy(plan, plan_at, plan_sem)
    plan_copy.start()

    gain_f = ln_gain[...].reshape(1, -1).astype(F32)
    bias_f = ln_bias[...].reshape(1, -1).astype(F32)
    bias[0:1, :] = proj_bias[...].reshape(1, -1).astype(F32)
    gains = rms_gain[...].reshape(1, -1).astype(F32)
    bias[1:2, :] = jnp.where(core == 0, gains[:, :half_cols], gains[:, half_cols:])

    def widen(first, values):
        for h in range(2):
            for b in range(blocks):
                at = pl.ds((first + 8 * h) * blocks + b, 8, stride=blocks)
                spread[at, :] = values[8 * h : 8 * h + 8, b * LANES : (b + 1) * LANES]

    def norm_copy(i):
        mine = normed.at[pl.ds(pl.multiple_of(core * half + i * part, part), part)]
        return pltpu.make_async_remote_copy(
            src_ref=mine,
            dst_ref=mine,
            send_sem=norm_send.at[i],
            recv_sem=norm_recv.at[i],
            device_id={"mp": peer},
            device_id_type=MESH,
        )

    for i in range(2):
        raw_copy(i).wait()
        if i == 0:
            for j in range(tiles1 // 2):
                w1_copy(j).start()
            for j in range(tiles2 // 2):
                w2_copy(j).start()

        @pl.loop(0, part // 16, unroll=4)
        def _(r):
            values = raw[pl.ds(pl.multiple_of(i * part + r * 16, 16), 16), :].astype(F32)
            centred = values - jnp.mean(values, axis=-1, keepdims=True)
            variance = jnp.mean(centred * centred, axis=-1, keepdims=True)
            scaled = centred * lax.rsqrt(variance + norm_epsilon) * gain_f + bias_f
            first = pl.multiple_of(core * half + i * part + r * 16, 16)
            normed[pl.ds(first, 16), :] = scaled.astype(BF16)
            widen(first, scaled)

        if i == 0:
            pl.semaphore_wait(barrier, senders)
        norm_copy(i).start()

    spread[rows * blocks :, :] = jnp.zeros((img_most * blocks, LANES), F32)
    squares[core] = jnp.zeros(squares.shape[1:], F32)

    here = tile_at == me * tiles_dev + own_tile
    my_col = lane_sum(jnp.where(here, counts_by, 0))
    my_off = lane_sum(jnp.where(here, earlier_by, 0))
    my_row = to_row(my_col)
    my_off_row = to_row(my_off)
    slot_row = to_row(slot)
    image_row, t_col = iota((TILE, images), 1), iota((TILE, images), 0)
    image_col, t_row = iota((images, TILE), 0), iota((images, TILE), 1)
    lane_at = iota((TILE, LANES), 1)
    for t in range(tiles_dev):
        hit = (image_row // img_tile == t) & (t_col >= my_off_row) & (t_col < my_off_row + my_row)
        box_at = lane_sum(jnp.where(hit, slot_row * img_most + (t_col - my_off_row) + 1, 0)) - 1
        off_at = lane_sum(jnp.where(hit, my_off_row + 1, 0)) - 1
        cols_at[t * TILE : (t + 1) * TILE, :] = jnp.where(lane_at == 0, box_at, off_at)
        hit = (image_col // img_tile == t) & (t_row >= my_off) & (t_row < my_off + my_col)
        rows_at[0:1, t * TILE : (t + 1) * TILE] = row_sum(jnp.where(hit, my_off + 1, 0)) - 1
        rows_at[1:2, t * TILE : (t + 1) * TILE] = row_sum(jnp.where(hit, t_row - my_off + 1, 0)) - 1
    meta = [
        pltpu.make_async_copy(cols_at, meta_cols, meta_sem.at[0]),
        pltpu.make_async_copy(rows_at, meta_rows, meta_sem.at[1]),
    ]
    for copy in meta:
        copy.start()

    plan_copy.wait()

    @pl.loop(0, slots, unroll=4)
    def _(i):
        first = plan_at[1, i]
        for h in range(img_most // 8):
            to = pl.ds(pl.multiple_of(i * img_most + 8 * h, 8), 8)
            cos_at[to, :] = table[pl.ds(first + 16 * h, 8, stride=2), :]
            sin_at[to, :] = table[pl.ds(first + 16 * h + 1, 8, stride=2), :]

    for i in range(2):
        norm_copy(i).wait_recv()

        @pl.loop(0, part // 16, unroll=2)
        def _(r):
            first = pl.multiple_of(peer * half + i * part + r * 16, 16)
            widen(first, normed[pl.ds(first, 16), :].astype(F32))

    def copy_hidden(c, p):
        cols = pl.ds(pl.multiple_of(core * half_cols + p * 2 * COL_TILE, COL_TILE), 2 * COL_TILE)
        ref = hidden.at[pl.ds(c * big, big), cols]
        return pltpu.make_async_remote_copy(
            src_ref=ref,
            dst_ref=ref,
            send_sem=hid_send.at[c * pairs + p],
            recv_sem=hid_recv.at[c * pairs + p],
            device_id={"mp": peer},
            device_id_type=MESH,
        )

    def copy_squares(c):
        ref = squares.at[core, pl.ds(c * big, big)]
        return pltpu.make_async_remote_copy(
            src_ref=ref,
            dst_ref=ref,
            send_sem=sq_send.at[c],
            recv_sem=sq_recv.at[c],
            device_id={"mp": peer},
            device_id_type=MESH,
        )

    def copy_block(o):
        at = pl.ds(o * block, block)
        return pltpu.make_async_remote_copy(
            src_ref=outbox.at[at],
            dst_ref=inbox.at[at],
            send_sem=a2a_send.at[o],
            recv_sem=a2a_recv.at[o],
            device_id={"dp": lax.rem(me + senders - order[o], senders)},
            device_id_type=MESH,
        )

    def own_copy():
        at = pl.ds(box_rows - block, block)
        return pltpu.make_async_copy(outbox.at[at], inbox.at[at], own_sem)

    def columns(j):
        return pl.ds(pl.multiple_of(j * COL_TILE, COL_TILE), COL_TILE)

    def project(c):
        @pl.loop(0, big // img_most, unroll=2)
        def _(i):
            first = plan_at[0, c * (big // img_most) + i]
            to = pl.ds(pl.multiple_of(i * img_most, img_most), img_most)
            for b in range(blocks):
                picked[to, b * LANES : (b + 1) * LANES] = jnp.concatenate(
                    [
                        spread[pl.ds(first + 8 * h * blocks + b, 8, stride=blocks), :]
                        for h in range(img_most // 8)
                    ],
                    axis=0,
                ).astype(BF16)

        if c == 0:
            for j in range(tiles1 // 2):
                w1_copy(j).wait()

        def multiply(j, slot):
            pre[slot] = jnp.dot(picked[...], w1[:, columns(j)], preferred_element_type=F32)

        def activate(j, slot):
            y = gelu(pre[slot] + bias[0:1, columns(j)])
            z = y * y
            total = z[:, :LANES]
            for b in range(1, COL_TILE // LANES):
                total = total + z[:, b * LANES : (b + 1) * LANES]
            squares[core, pl.ds(c * big, big), :] += total
            to = pl.ds(pl.multiple_of(core * half_cols + j * COL_TILE, COL_TILE), COL_TILE)
            hidden[pl.ds(c * big, big), to] = (y * bias[1:2, columns(j)]).astype(BF16)

        multiply(0, 0)

        @pl.loop(0, pairs - 1)
        def _(i):
            multiply(2 * i + 1, 1)
            activate(2 * i, 0)
            multiply(2 * i + 2, 0)
            activate(2 * i + 1, 1)
            copy_hidden(c, i).start()

        multiply(tiles1 - 1, 1)
        activate(tiles1 - 2, 0)
        activate(tiles1 - 1, 1)
        copy_squares(c).start()
        copy_hidden(c, pairs - 1).start()

    wide_at = iota((img_most, QUERY_PER_KEY * TILE), 1)
    causal = iota((img_most, QUERY_PER_KEY * TILE), 0) <= wide_at % img_most
    own_image = (wide_at % TILE) // img_most
    w = HEAD_SIZE

    def qkv(c):
        here = pl.ds(c * CHUNK, CHUNK)
        fresh = c * CHUNK % big == 0
        if c == 0:
            for j in range(tiles2 // 2):
                w2_copy(j).wait()
        if fresh:
            mine = pl.ds(pl.multiple_of(core * half_cols, half_cols), half_cols)
            other = pl.ds(pl.multiple_of(peer * half_cols, half_cols), half_cols)

            @pl.loop(0, tiles2 // 2)
            def _(j):
                cols = pl.ds(pl.multiple_of(j * 2 * COL_TILE, COL_TILE), 2 * COL_TILE)
                proj[:, cols] = jnp.dot(hidden[here, mine], w2[mine, cols], preferred_element_type=F32)

            copy_squares(c * CHUNK // big).wait_recv()
            for p in range(pairs):
                copy_hidden(c * CHUNK // big, p).wait_recv()

            @pl.loop(0, tiles2 // 2)
            def _(j):
                cols = pl.ds(pl.multiple_of(j * 2 * COL_TILE, COL_TILE), 2 * COL_TILE)
                proj[:, cols] += jnp.dot(
                    hidden[here, other], w2[other, cols], preferred_element_type=F32
                )
        else:

            @pl.loop(0, tiles2 // 2)
            def _(j):
                cols = pl.ds(pl.multiple_of(j * 2 * COL_TILE, COL_TILE), 2 * COL_TILE)
                proj[:, cols] = jnp.dot(hidden[here, :], w2[:, cols], preferred_element_type=F32)

    def attend(c):
        for first in range(0, CHUNK, TILE):
            to = pl.ds(c * CHUNK + first, TILE)
            total = lane_sum(squares[0, to, :] + squares[1, to, :])
            scale = lax.rsqrt(total * (1.0 / (2 * half_cols)) + rms_epsilon)
            cos = cos_at[to, :] * scale
            sin = sin_at[to, :] * scale

            def head(h):
                return proj[first : first + TILE, h * w : (h + 1) * w]

            def turned(h):
                v = head(h)
                return (v * cos + pltpu.roll(v, w // 2, 1) * sin).astype(BF16)

            seen = []
            for g in range(groups):
                h0 = g * (QUERY_PER_KEY + 2)
                q = jnp.concatenate([turned(h0 + i) for i in range(QUERY_PER_KEY)], axis=0)
                k = turned(h0 + QUERY_PER_KEY)
                outbox[to, (g + 1) * w : (g + 2) * w] = (head(h0 + QUERY_PER_KEY + 1) * scale).astype(BF16)
                scores = lax.dot_general(
                    k, q, (((1,), (1,)), ((), ())), preferred_element_type=F32
                )
                kept = scores[:img_most]
                for j in range(1, img_tile):
                    kept = jnp.where(own_image == j, scores[j * img_most : (j + 1) * img_most], kept)
                kept = jnp.where(causal, kept * np.float32(HEAD_SIZE ** (-0.5)), -1e30)
                weights = jnp.exp(kept - jnp.max(kept, axis=0, keepdims=True))
                probs = weights / row_sum(weights)
                seen += [probs[:, i * TILE : (i + 1) * TILE] for i in range(QUERY_PER_KEY)]
            outbox[to, :w] = jnp.concatenate(seen, axis=0).T.astype(BF16)
            for o in range((c * CHUNK + first) // block, (c * CHUNK + first + TILE) // block):
                if o < senders - 1:
                    copy_block(o).start()
                else:
                    own_copy().start()

    for c in range(bigs):
        project(c)
    for c in range(chunks):
        qkv(c)
        attend(c)

    for o in range(senders - 1):
        copy_block(o).wait_recv()
    own_copy().wait()
    for copy in meta:
        copy.wait()
    for i in range(2):
        norm_copy(i).wait_send()
    for c in range(bigs):
        copy_squares(c).wait_send()
        for p in range(pairs):
            copy_hidden(c, p).wait_send()
    for o in range(senders - 1):
        copy_block(o).wait_send()


def place_kernel(heads, img_most, meta_cols, meta_rows, box, out, placed, out_sem):
    box_rows = box.shape[0]
    groups = heads // QUERY_PER_KEY
    w = HEAD_SIZE
    tiles = out.shape[0] // TILE

    def out_copy(t):
        at = pl.ds(t * TILE, TILE)
        return pltpu.make_async_copy(placed.at[at], out.at[at], out_sem.at[t])

    key_at = iota((heads * img_most, TILE), 0)
    for t in range(tiles):
        at = slice(t * TILE, (t + 1) * TILE)
        select = jnp.where(iota((TILE, box_rows), 1) == meta_cols[at, 0:1], 1.0, 0.0).astype(BF16)
        got = jnp.dot(select, box[...], preferred_element_type=F32).astype(BF16)
        inside = meta_rows[1:2, at]
        expand = jnp.concatenate(
            [jnp.where(key_at == h * img_most + inside, 1.0, 0.0).astype(BF16) for h in range(heads)],
            axis=1,
        )
        probs = jnp.dot(got[:, : heads * img_most], expand, preferred_element_type=F32)
        same = meta_cols[at, 1:2] == meta_rows[0:1, at]
        for g in range(groups):
            seen = jnp.concatenate(
                [
                    jnp.where(same, probs[:, h * TILE : (h + 1) * TILE], 0.0).astype(BF16)
                    for h in range(g * QUERY_PER_KEY, (g + 1) * QUERY_PER_KEY)
                ],
                axis=0,
            )
            values = got[:, heads * img_most + g * w : heads * img_most + (g + 1) * w]
            attended = jnp.dot(seen, values, preferred_element_type=F32).astype(BF16)
            for i in range(QUERY_PER_KEY):
                a = (g * QUERY_PER_KEY + i) * w
                placed[at, a : a + w] = attended[i * TILE : (i + 1) * TILE]
        out_copy(t).start()
    for t in range(tiles):
        out_copy(t).wait()


def local(
    patches, ln_gain, ln_bias, w_proj, proj_bias, rms_gain, w_qkv, image_counts, source_shift
):
    senders = lax.axis_size("dp")
    order = shift_order(senders)
    half, d_vit = patches.shape
    rows = 2 * half
    half_cols = w_proj.shape[1]
    qkv_cols = w_qkv.shape[1]
    groups = qkv_cols // ((QUERY_PER_KEY + 2) * HEAD_SIZE)
    heads = groups * QUERY_PER_KEY
    out_cols = heads * HEAD_SIZE
    images = source_shift.shape[0]
    img_most = TILE // (images // (rows // TILE))
    pair_slots = (images + senders - 1) // senders
    box_rows = senders * pair_slots * img_most
    box_cols = heads * img_most + groups * HEAD_SIZE
    big = min(PROJECT_ROWS, box_rows)
    bigs = box_rows // big
    pairs = half_cols // COL_TILE // 2
    vmem = pl.BlockSpec(memory_space=pltpu.VMEM)
    hbm = pl.BlockSpec(memory_space=pl.ANY)
    dma = pltpu.SemaphoreType.DMA
    box, cols, lines = pl.pallas_call(
        functools.partial(kernel, senders, order),
        out_shape=[
            jax.ShapeDtypeStruct((box_rows, box_cols), BF16),
            jax.ShapeDtypeStruct((rows, LANES), I32),
            jax.ShapeDtypeStruct((8, rows), I32),
        ],
        in_specs=[vmem] * 7 + [hbm] * 3,
        out_specs=[hbm] * 3,
        scratch_shapes=[
            pltpu.VMEM((half, d_vit), BF16),
            pltpu.VMEM(w_proj.shape, BF16),
            pltpu.VMEM(w_qkv.shape, BF16),
            pltpu.VMEM((rows, d_vit), BF16),
            pltpu.VMEM(((rows + img_most) * (d_vit // LANES), LANES), F32),
            pltpu.VMEM((big, d_vit), BF16),
            pltpu.VMEM((box_rows, 2 * half_cols), BF16),
            pltpu.VMEM((2, box_rows, LANES), F32),
            pltpu.VMEM((2, big, COL_TILE), F32),
            pltpu.VMEM((2, half_cols), F32),
            pltpu.VMEM((CHUNK, qkv_cols), F32),
            pltpu.VMEM((box_rows, HEAD_SIZE), F32),
            pltpu.VMEM((box_rows, HEAD_SIZE), F32),
            pltpu.VMEM((box_rows, box_cols), BF16),
            pltpu.VMEM((rows, LANES), I32),
            pltpu.VMEM((8, rows), I32),
            pltpu.VMEM((8, LANES), I32),
            pltpu.SMEM((8, LANES), I32),
            dma((2,)),
            dma((half_cols // COL_TILE // 2,)),
            dma((qkv_cols // COL_TILE // 2,)),
            dma,
            dma((2,)),
            dma,
            dma((2,)),
            dma((2,)),
            dma((bigs * pairs,)),
            dma((bigs * pairs,)),
            dma((bigs,)),
            dma((bigs,)),
            dma((senders,)),
            dma((senders,)),
        ],
        compiler_params=pltpu.CompilerParams(
            collective_id=0, has_side_effects=True, vmem_limit_bytes=60 * 1024 * 1024
        ),
        name="projector_attention",
    )(
        ln_gain,
        ln_bias,
        proj_bias,
        rms_gain,
        image_counts.T,
        source_shift,
        jnp.asarray(rotary_table(TILE + img_most)),
        patches,
        w_proj,
        w_qkv,
    )
    return pl.pallas_call(
        functools.partial(place_kernel, heads, img_most),
        out_shape=jax.ShapeDtypeStruct((rows, out_cols), BF16),
        in_specs=[vmem] * 3,
        out_specs=hbm,
        scratch_shapes=[pltpu.VMEM((rows, out_cols), BF16), dma((rows // TILE,))],
        name="place",
    )(cols, lines, box)


def solution(mesh):
    in_specs = (
        P(("dp", "mp"), None),
        P(),
        P(),
        P(None, "mp"),
        P("mp"),
        P(),
        P(None, "mp"),
        P(),
        P(),
    )
    out_specs = P("dp", "mp")
    return jax.shard_map(local, mesh=mesh, in_specs=in_specs, out_specs=out_specs, check_vma=False)
```

time: 59.9 us -> 42.8 us (0.71)
  Pallas kernels: 57.5 us -> 42.6 us
  local copies, waits for them, and re-layouts: 2.26 us -> 0 us
    pallas_call x1 -> x2, Pallas kernels: 57.5 us -> 42.6 us  [the longest x1 39 us: local(): pl.pallas_call(functools.partial(kernel, senders, order), out_shape=[jax....]
    unnamed x1 -> x0, local copies, waits for them, and re-layouts: 2.26 us -> none
where the time goes in v1:
time: 42.8 us; the launch traced here: 42.6 us
  Pallas kernels  42.6 us (100%)
    pallas_call x1, Pallas kernels, local(): pl.pallas_call(functools.partial(kernel, senders, order), out_shape=[jax....  39 us
    pallas_call x1, Pallas kernels, local(): pl.pallas_call(functools.partial(place_kernel, heads, img_most), out_shap...  3.58 us

profile of v1, /device:TPU:0, one launch (start us, length us, event | category | flops | bytes accessed | tf_op | source)
XLA Modules:
  0.0 42.6 jit_solution(9118748781081018666)
XLA Ops:
  0.0 39.0 %projector_attention.1 = (bf16[512,384]{1,0:T(8,128)(2,1)}, s32[512,128]{1,0:T(8,128)}, s32[8,512]{1,0:T(8,128)}) custom-call(bf16[3200]{0:T(1024)(128)(2,1)} %ln_gain.1, bf16[3200]{0:T(1024)(128)(2,1)} %ln_bias.1, bf16[2048]{0:T(1024)(128)(2,1)} %proj_bias.1, bf16[4096]{0:T(1024)(128)(2,1)} %rms_gain.1, s32[8,64]{1,0:T(8,128)} %bitcast.1, s32[32]{0:T(128)} %source_shift.1, ...), custom_call_target="tpu_custom_call" | custom-call | tf_op jit(solution)/shard_map/projector_attention/pallas_call | solution.py:533
  39.0 3.6 %place.1 = bf16[512,1024]{1,0:T(8,128)(2,1)} custom-call(s32[512,128]{1,0:T(8,128)} %get-tuple-element.8.meta_cols, s32[8,512]{1,0:T(8,128)} %get-tuple-element.9.meta_rows, bf16[512,384]{1,0:T(8,128)(2,1)} %get-tuple-element.10.box), custom_call_target="tpu_custom_call" | custom-call | tf_op jit(solution)/shard_map/place/pallas_call | solution.py:592

commit v2 on v1

v2 whole, which is shorter than its diff:
```python
import functools

import jax
import jax.numpy as jnp
import numpy as np
from jax import lax
from jax.experimental import pallas as pl
from jax.experimental.pallas import tpu as pltpu
from jax.sharding import PartitionSpec as P

HEAD_SIZE = 128
TILE = 128
QUERY_PER_KEY = 4
COL_TILE = 512
LANES = 128
CHUNK = 256

norm_epsilon = 1e-05
rms_epsilon = 1e-05
rotary_base = 500000.0

F32 = jnp.float32
BF16 = jnp.bfloat16
I32 = jnp.int32
MESH = pl.DeviceIdType.MESH


def shift_order(senders):
    return sorted(range(senders), key=lambda v: (abs(v - senders // 2), v))


def rotary_table(positions):
    frequency = np.float32(rotary_base) ** (
        -(np.arange(HEAD_SIZE // 2, dtype=np.float32) * np.float32(2.0 / HEAD_SIZE))
    )
    angles = np.arange(positions, dtype=np.float32)[:, None] * frequency[None, :].astype(np.float32)
    cos = np.cos(angles.astype(np.float64)).astype(np.float32)
    sin = np.sin(angles.astype(np.float64)).astype(np.float32)
    both = np.stack([np.concatenate([cos, cos], 1), np.concatenate([-sin, sin], 1)], axis=1)
    return both.reshape(2 * positions, HEAD_SIZE)


def gelu(v):
    return 0.5 * v * (1.0 + lax.erf(v * np.float32(0.5**0.5)))


def iota(shape, axis):
    return lax.broadcasted_iota(jnp.int32, shape, axis)


def lane_sum(x):
    return jnp.sum(x, axis=1, keepdims=True)


def row_sum(x):
    return jnp.sum(x, axis=0, keepdims=True)


def kernel(
    senders,
    order,
    ln_gain_in,
    ln_bias_in,
    proj_bias_in,
    rms_gain_in,
    counts_in,
    source_shift_in,
    table_in,
    patches,
    w_proj,
    w_qkv,
    box_probs,
    box_values,
    meta_cols,
    meta_rows,
    ln_gain,
    ln_bias,
    proj_bias,
    rms_gain,
    counts,
    source_shift,
    table,
    raw,
    w1,
    w2,
    normed,
    spread,
    picked,
    hidden,
    squares,
    bias,
    proj,
    cos_at,
    sin_at,
    probs_at,
    values_at,
    cols_at,
    rows_at,
    plan,
    plan_at,
    small_sem,
    raw_sem,
    w1_sem,
    w2_sem,
    plan_sem,
    meta_sem,
    norm_send,
    norm_recv,
    hid_send,
    hid_recv,
    sq_send,
    sq_recv,
    probs_send,
    probs_recv,
    values_send,
    values_recv,
):
    me = lax.axis_index("dp")
    core = lax.axis_index("mp")
    peer = 1 - core
    half, d_vit = raw.shape
    rows = 2 * half
    blocks = d_vit // LANES
    box_rows = values_at.shape[0]
    block = box_rows // senders
    images = source_shift.shape[0]
    tiles_dev = rows // TILE
    img_tile = images // tiles_dev
    img_most = TILE // img_tile
    slots = box_rows // img_most
    pair_slots = block // img_most
    half_cols = w_proj.shape[1]
    qkv_cols = w_qkv.shape[1]
    groups = qkv_cols // ((QUERY_PER_KEY + 2) * HEAD_SIZE)
    tiles1 = half_cols // COL_TILE
    qk_group = (QUERY_PER_KEY + 1) * HEAD_SIZE
    qk_cols = groups * qk_group
    chunks = box_rows // CHUNK
    part = 64
    parts = half // part

    def raw_copy(i):
        at = pl.ds(i * part, part)
        return pltpu.make_async_copy(patches.at[at], raw.at[at], raw_sem.at[i])

    def w1_copy(j):
        cols = pl.ds(j * COL_TILE, COL_TILE)
        return pltpu.make_async_copy(w_proj.at[:, cols], w1.at[:, cols], w1_sem.at[j])

    def w2_copy(j):
        g = j // 2
        first = g * (qk_group + HEAD_SIZE)
        if j % 2 == 0:
            source, to, width = first, g * qk_group, qk_group
        else:
            source, to, width = first + qk_group, qk_cols + g * HEAD_SIZE, HEAD_SIZE
        return pltpu.make_async_copy(
            w_qkv.at[:, pl.ds(source, width)], w2.at[:, pl.ds(to, width)], w2_sem.at[j]
        )

    smalls = [
        pltpu.make_async_copy(there, here, small_sem.at[i])
        for i, (there, here) in enumerate(
            [
                (counts_in, counts),
                (source_shift_in, source_shift),
                (ln_gain_in, ln_gain),
                (ln_bias_in, ln_bias),
                (proj_bias_in, proj_bias),
                (rms_gain_in, rms_gain),
                (table_in, table),
            ]
        )
    ]
    for copy in smalls[:2]:
        copy.start()
    for i in range(parts):
        raw_copy(i).start()
    for copy in smalls[2:]:
        copy.start()

    barrier = pltpu.get_barrier_semaphore()
    pl.semaphore_signal(barrier, inc=1, device_id={"mp": peer}, device_id_type=MESH)
    for v in range(1, senders):
        pl.semaphore_signal(
            barrier, inc=1, device_id={"dp": lax.rem(me + v, senders)}, device_id_type=MESH
        )

    for copy in smalls[:2]:
        copy.wait()
    sq = (images, images)
    k_at, l_at = iota(sq, 0), iota(sq, 1)
    eye = k_at == l_at
    before = l_at < k_at

    def to_row(col):
        return row_sum(jnp.where(eye, col, 0))

    def to_col(row):
        return lane_sum(jnp.where(eye, row, 0))

    tiles_all = counts.shape[1]
    image_counts = counts[...]
    earlier = jnp.zeros((img_tile, tiles_all), I32)
    for j in range(img_tile - 1):
        earlier += jnp.where(iota((img_tile, tiles_all), 0) > j, image_counts[j : j + 1, :], 0)
    counts_by = jnp.concatenate([image_counts] * tiles_dev, axis=0)
    earlier_by = jnp.concatenate([earlier] * tiles_dev, axis=0)
    tile_at = iota((images, tiles_all), 1)
    own_tile = iota((images, 1), 0) // img_tile

    shift_row = source_shift[...].reshape(1, images)
    shift = to_col(shift_row)
    dest = me - shift
    dest = jnp.where(dest < 0, dest + senders, dest)
    place = jnp.zeros((images, 1), I32)
    for v in range(senders):
        place = jnp.where(shift == order[v], v, place)
    there = tile_at == dest * tiles_dev + own_tile
    starts = lane_sum(jnp.where(before, to_row(lane_sum(jnp.where(there, counts_by, 0))), 0))
    far_offset = lane_sum(jnp.where(there, earlier_by, 0))
    rank = lane_sum(jnp.where(before & (shift_row == shift), 1, 0))
    slot = place * pair_slots + rank

    slot_hit = slot == iota((images, LANES), 1)
    plan[0:1, :] = row_sum(jnp.where(slot_hit, starts * blocks, 0))
    plan[1:2, :] = row_sum(jnp.where(slot_hit, far_offset * 2, 0))
    plan_copy = pltpu.make_async_copy(plan, plan_at, plan_sem)
    plan_copy.start()

    for copy in smalls[2:]:
        copy.wait()
    gain_f = ln_gain[...].reshape(1, -1).astype(F32)
    bias_f = ln_bias[...].reshape(1, -1).astype(F32)
    bias[0:1, :] = proj_bias[...].reshape(1, -1).astype(F32)
    gains = rms_gain[...].reshape(1, -1).astype(F32)
    bias[1:2, :] = jnp.where(core == 0, gains[:, :half_cols], gains[:, half_cols:])

    def widen(first, values):
        for h in range(2):
            for b in range(blocks):
                at = pl.ds((first + 8 * h) * blocks + b, 8, stride=blocks)
                spread[at, :] = values[8 * h : 8 * h + 8, b * LANES : (b + 1) * LANES]

    def norm_copy(i):
        mine = normed.at[pl.ds(pl.multiple_of(core * half + i * part, part), part)]
        return pltpu.make_async_remote_copy(
            src_ref=mine,
            dst_ref=mine,
            send_sem=norm_send.at[i],
            recv_sem=norm_recv.at[i],
            device_id={"mp": peer},
            device_id_type=MESH,
        )

    for i in range(parts):
        raw_copy(i).wait()
        if i == 0:
            for j in range(tiles1):
                w1_copy(j).start()

        @pl.loop(0, part // 16, unroll=4)
        def _(r):
            values = raw[pl.ds(pl.multiple_of(i * part + r * 16, 16), 16), :].astype(F32)
            centred = values - jnp.mean(values, axis=-1, keepdims=True)
            variance = jnp.mean(centred * centred, axis=-1, keepdims=True)
            scaled = centred * lax.rsqrt(variance + norm_epsilon) * gain_f + bias_f
            first = pl.multiple_of(core * half + i * part + r * 16, 16)
            normed[pl.ds(first, 16), :] = scaled.astype(BF16)
            widen(first, scaled)

        if i == 0:
            pl.semaphore_wait(barrier, senders)
        norm_copy(i).start()

    spread[rows * blocks :, :] = jnp.zeros((img_most * blocks, LANES), F32)

    here = tile_at == me * tiles_dev + own_tile
    my_col = lane_sum(jnp.where(here, counts_by, 0))
    my_off = lane_sum(jnp.where(here, earlier_by, 0))
    my_row = to_row(my_col)
    my_off_row = to_row(my_off)
    slot_row = to_row(slot)
    image_row, t_col = iota((TILE, images), 1), iota((TILE, images), 0)
    image_col, t_row = iota((images, TILE), 0), iota((images, TILE), 1)
    lane_at = iota((TILE, LANES), 1)
    for t in range(tiles_dev):
        hit = (image_row // img_tile == t) & (t_col >= my_off_row) & (t_col < my_off_row + my_row)
        box_at = lane_sum(jnp.where(hit, slot_row * img_most + (t_col - my_off_row) + 1, 0)) - 1
        off_at = lane_sum(jnp.where(hit, my_off_row + 1, 0)) - 1
        cols_at[t * TILE : (t + 1) * TILE, :] = jnp.where(lane_at == 0, box_at, off_at)
        hit = (image_col // img_tile == t) & (t_row >= my_off) & (t_row < my_off + my_col)
        rows_at[0:1, t * TILE : (t + 1) * TILE] = row_sum(jnp.where(hit, my_off + 1, 0)) - 1
        rows_at[1:2, t * TILE : (t + 1) * TILE] = row_sum(jnp.where(hit, t_row - my_off + 1, 0)) - 1
    meta = [
        pltpu.make_async_copy(cols_at, meta_cols, meta_sem.at[0]),
        pltpu.make_async_copy(rows_at, meta_rows, meta_sem.at[1]),
    ]
    for copy in meta:
        copy.start()

    plan_copy.wait()

    @pl.loop(0, slots, unroll=4)
    def _(i):
        first = plan_at[1, i]
        for h in range(img_most // 8):
            to = pl.ds(pl.multiple_of(i * img_most + 8 * h, 8), 8)
            cos_at[to, :] = table[pl.ds(first + 16 * h, 8, stride=2), :]
            sin_at[to, :] = table[pl.ds(first + 16 * h + 1, 8, stride=2), :]

    for i in range(parts):
        norm_copy(i).wait_recv()

        @pl.loop(0, part // 16, unroll=2)
        def _(r):
            first = pl.multiple_of(peer * half + i * part + r * 16, 16)
            widen(first, normed[pl.ds(first, 16), :].astype(F32))

    mine = pl.ds(pl.multiple_of(core * half_cols, half_cols), half_cols)

    def to_peer(ref, send_sem, recv_sem):
        return pltpu.make_async_remote_copy(
            src_ref=ref,
            dst_ref=ref,
            send_sem=send_sem,
            recv_sem=recv_sem,
            device_id={"mp": peer},
            device_id_type=MESH,
        )

    def copy_hidden(c):
        return to_peer(hidden.at[pl.ds(c * CHUNK, CHUNK), mine], hid_send.at[c], hid_recv.at[c])

    def copy_squares(c):
        return to_peer(squares.at[core, pl.ds(c * CHUNK, CHUNK)], sq_send.at[c], sq_recv.at[c])

    def exchange(o, outbox, inbox, send_sem, recv_sem):
        at = pl.ds(o * block, block)
        if o == senders - 1:
            return pltpu.make_async_copy(outbox.at[at], inbox.at[at], send_sem.at[o])
        return pltpu.make_async_remote_copy(
            src_ref=outbox.at[at],
            dst_ref=inbox.at[at],
            send_sem=send_sem.at[o],
            recv_sem=recv_sem.at[o],
            device_id={"dp": lax.rem(me + senders - order[o], senders)},
            device_id_type=MESH,
        )

    def copy_probs(o):
        return exchange(o, probs_at, box_probs, probs_send, probs_recv)

    def copy_values(o):
        return exchange(o, values_at, box_values, values_send, values_recv)


    @pl.loop(0, slots, unroll=2)
    def _(i):
        first = plan_at[0, i]
        to = pl.ds(pl.multiple_of(i * img_most, img_most), img_most)
        for b in range(blocks):
            picked[to, b * LANES : (b + 1) * LANES] = jnp.concatenate(
                [
                    spread[pl.ds(first + 8 * h * blocks + b, 8, stride=blocks), :]
                    for h in range(img_most // 8)
                ],
                axis=0,
            ).astype(BF16)

    def project(c):
        at = pl.ds(c * CHUNK, CHUNK)
        for j in range(tiles1):
            if c == 0 and j % 2 == 0:
                w1_copy(j).wait()
                w1_copy(j + 1).wait()
                if j + 2 == tiles1:
                    for g in range(2 * groups):
                        w2_copy(g).start()
            cols = slice(j * COL_TILE, (j + 1) * COL_TILE)
            pre = jnp.dot(picked[at, :], w1[:, cols], preferred_element_type=F32)
            y = gelu(pre + bias[0:1, cols])
            z = y * y
            total = z[:, :LANES]
            for b in range(1, COL_TILE // LANES):
                total = total + z[:, b * LANES : (b + 1) * LANES]
            if j == 0:
                squares[core, at, :] = total
            else:
                squares[core, at, :] += total
            to = pl.ds(pl.multiple_of(core * half_cols + j * COL_TILE, COL_TILE), COL_TILE)
            hidden[at, to] = (y * bias[1:2, cols]).astype(BF16)
        copy_squares(c).start()
        copy_hidden(c).start()

    wide_at = iota((img_most, QUERY_PER_KEY * TILE), 1)
    causal = iota((img_most, QUERY_PER_KEY * TILE), 0) <= wide_at % img_most
    own_image = (wide_at % TILE) // img_most
    w = HEAD_SIZE

    def product(c, cols):
        return jnp.dot(hidden[pl.ds(c * CHUNK, CHUNK), :], w2[:, cols], preferred_element_type=F32)

    qk_tiles = [slice(f, min(f + COL_TILE, qk_cols)) for f in range(0, qk_cols, COL_TILE)]

    def qk(c, j):
        proj[c % 2, :, qk_tiles[j]] = product(c, qk_tiles[j])

    def values(c):
        at = pl.ds(c * CHUNK, CHUNK)
        copy_squares(c).wait_recv()
        copy_hidden(c).wait_recv()
        if c == 0:
            for j in range(2 * groups):
                w2_copy(j).wait()
        total = lane_sum(squares[0, at, :] + squares[1, at, :])
        scale = lax.rsqrt(total * (1.0 / (2 * half_cols)) + rms_epsilon)
        value_rows = product(c, slice(qk_cols, qkv_cols))
        qk(c, 0)
        values_at[at, :] = (value_rows * scale).astype(BF16)
        cos_at[at, :] *= scale
        sin_at[at, :] *= scale
        for o in range(c * CHUNK // block, (c + 1) * CHUNK // block):
            copy_values(o).start()

    def attend(c, first):
        to = pl.ds(c * CHUNK + first, TILE)
        cos = cos_at[to, :]
        sin = sin_at[to, :]

        def turned(h):
            v = proj[c % 2, first : first + TILE, h * w : (h + 1) * w]
            return (v * cos + pltpu.roll(v, w // 2, 1) * sin).astype(BF16)

        seen = []
        for g in range(groups):
            h0 = g * (QUERY_PER_KEY + 1)
            q = jnp.concatenate([turned(h0 + i) for i in range(QUERY_PER_KEY)], axis=0)
            k = turned(h0 + QUERY_PER_KEY)
            scores = lax.dot_general(
                k, q, (((1,), (1,)), ((), ())), preferred_element_type=F32
            )
            kept = scores[:img_most]
            for j in range(1, img_tile):
                kept = jnp.where(own_image == j, scores[j * img_most : (j + 1) * img_most], kept)
            kept = jnp.where(causal, kept * np.float32(HEAD_SIZE ** (-0.5)), -1e30)
            weights = jnp.exp(kept - jnp.max(kept, axis=0, keepdims=True))
            probs = weights / row_sum(weights)
            seen += [probs[:, i * TILE : (i + 1) * TILE] for i in range(QUERY_PER_KEY)]
        probs_at[to, :] = jnp.concatenate(seen, axis=0).T.astype(BF16)
        for o in range((c * CHUNK + first) // block, (c * CHUNK + first + TILE) // block):
            copy_probs(o).start()

    tiles = CHUNK // TILE
    project(0)
    if chunks > 1:
        project(1)
    values(0)
    for j in range(1, len(qk_tiles)):
        qk(0, j)
    for c in range(chunks):
        if c + 2 < chunks:
            project(c + 2)
        if c + 1 < chunks:
            values(c + 1)
        for j in range(max(tiles, len(qk_tiles))):
            if c + 1 < chunks and j + 1 < len(qk_tiles):
                qk(c + 1, j + 1)
            if j < tiles:
                attend(c, j * TILE)

    for copy in (copy_values, copy_probs):
        for o in range(senders - 1):
            copy(o).wait_recv()
        copy(senders - 1).wait()
    for copy in meta:
        copy.wait()
    for i in range(parts):
        norm_copy(i).wait_send()
    for c in range(chunks):
        copy_squares(c).wait_send()
        copy_hidden(c).wait_send()
    for copy in (copy_values, copy_probs):
        for o in range(senders - 1):
            copy(o).wait_send()


def place_kernel(heads, img_most, *refs):
    cols_in, rows_in, probs_in, values_in, out, meta_cols, meta_rows, box, placed, in_sem, out_sem = refs
    box_rows, prob_cols = probs_in.shape
    loads = [
        pltpu.make_async_copy(there, here, in_sem.at[i])
        for i, (there, here) in enumerate(
            [
                (cols_in, meta_cols),
                (rows_in, meta_rows),
                (probs_in, box.at[:, pl.ds(0, prob_cols)]),
                (values_in, box.at[:, pl.ds(prob_cols, values_in.shape[1])]),
            ]
        )
    ]
    for copy in loads:
        copy.start()
    for copy in loads:
        copy.wait()
    groups = heads // QUERY_PER_KEY
    w = HEAD_SIZE
    tiles = out.shape[0] // TILE

    def out_copy(t):
        at = pl.ds(t * TILE, TILE)
        return pltpu.make_async_copy(placed.at[at], out.at[at], out_sem.at[t])

    key_at = iota((heads * img_most, TILE), 0)
    ats = [slice(t * TILE, (t + 1) * TILE) for t in range(tiles)]
    slot_at = iota((TILE, box_rows), 1)
    selects = [jnp.where(slot_at == meta_cols[at, 0:1], 1.0, 0.0).astype(BF16) for at in ats]
    own = [
        jnp.dot(select, box[...], preferred_element_type=F32).astype(BF16) for select in selects
    ]
    expanded = []
    for t, at in enumerate(ats):
        inside = meta_rows[1:2, at]
        expand = jnp.concatenate(
            [jnp.where(key_at == h * img_most + inside, 1.0, 0.0).astype(BF16) for h in range(heads)],
            axis=1,
        )
        expanded.append(jnp.dot(own[t][:, :prob_cols], expand, preferred_element_type=F32))
    for t, at in enumerate(ats):
        same = meta_cols[at, 1:2] == meta_rows[0:1, at]
        for g in range(groups):
            seen = jnp.concatenate(
                [
                    jnp.where(same, expanded[t][:, h * TILE : (h + 1) * TILE], 0.0).astype(BF16)
                    for h in range(g * QUERY_PER_KEY, (g + 1) * QUERY_PER_KEY)
                ],
                axis=0,
            )
            values = own[t][:, prob_cols + g * w : prob_cols + (g + 1) * w]
            attended = jnp.dot(seen, values, preferred_element_type=F32).astype(BF16)
            for i in range(QUERY_PER_KEY):
                a = (g * QUERY_PER_KEY + i) * w
                placed[at, a : a + w] = attended[i * TILE : (i + 1) * TILE]
        if t % 2 == 1:
            out_copy(t - 1).start()
            out_copy(t).start()
    for t in range(tiles):
        out_copy(t).wait()


def local(
    patches, ln_gain, ln_bias, w_proj, proj_bias, rms_gain, w_qkv, image_counts, source_shift
):
    senders = lax.axis_size("dp")
    order = shift_order(senders)
    half, d_vit = patches.shape
    rows = 2 * half
    parts = half // 64
    half_cols = w_proj.shape[1]
    qkv_cols = w_qkv.shape[1]
    groups = qkv_cols // ((QUERY_PER_KEY + 2) * HEAD_SIZE)
    heads = groups * QUERY_PER_KEY
    out_cols = heads * HEAD_SIZE
    images = source_shift.shape[0]
    img_most = TILE // (images // (rows // TILE))
    pair_slots = (images + senders - 1) // senders
    box_rows = senders * pair_slots * img_most
    prob_cols, value_cols = heads * img_most, groups * HEAD_SIZE
    chunks = box_rows // CHUNK
    hbm = pl.BlockSpec(memory_space=pl.ANY)
    dma = pltpu.SemaphoreType.DMA
    smalls = (
        ln_gain,
        ln_bias,
        proj_bias,
        rms_gain,
        image_counts.T,
        source_shift,
        jnp.asarray(rotary_table(TILE + img_most)),
    )
    probs, values, cols, lines = pl.pallas_call(
        functools.partial(kernel, senders, order),
        out_shape=[
            jax.ShapeDtypeStruct((box_rows, prob_cols), BF16),
            jax.ShapeDtypeStruct((box_rows, value_cols), BF16),
            jax.ShapeDtypeStruct((rows, LANES), I32),
            jax.ShapeDtypeStruct((8, rows), I32),
        ],
        in_specs=[hbm] * 10,
        out_specs=[hbm] * 4,
        scratch_shapes=[
            *[pltpu.VMEM(x.shape, x.dtype) for x in smalls],
            pltpu.VMEM((half, d_vit), BF16),
            pltpu.VMEM(w_proj.shape, BF16),
            pltpu.VMEM(w_qkv.shape, BF16),
            pltpu.VMEM((rows, d_vit), BF16),
            pltpu.VMEM(((rows + img_most) * (d_vit // LANES), LANES), F32),
            pltpu.VMEM((box_rows, d_vit), BF16),
            pltpu.VMEM((box_rows, 2 * half_cols), BF16),
            pltpu.VMEM((2, box_rows, LANES), F32),
            pltpu.VMEM((2, half_cols), F32),
            pltpu.VMEM((2, CHUNK, qkv_cols - value_cols), F32),
            pltpu.VMEM((box_rows, HEAD_SIZE), F32),
            pltpu.VMEM((box_rows, HEAD_SIZE), F32),
            pltpu.VMEM((box_rows, prob_cols), BF16),
            pltpu.VMEM((box_rows, value_cols), BF16),
            pltpu.VMEM((rows, LANES), I32),
            pltpu.VMEM((8, rows), I32),
            pltpu.VMEM((8, LANES), I32),
            pltpu.SMEM((8, LANES), I32),
            dma((len(smalls),)),
            dma((parts,)),
            dma((half_cols // COL_TILE,)),
            dma((2 * groups,)),
            dma,
            dma((2,)),
            dma((parts,)),
            dma((parts,)),
            dma((chunks,)),
            dma((chunks,)),
            dma((chunks,)),
            dma((chunks,)),
            dma((senders,)),
            dma((senders,)),
            dma((senders,)),
            dma((senders,)),
        ],
        compiler_params=pltpu.CompilerParams(
            collective_id=0, has_side_effects=True, vmem_limit_bytes=60 * 1024 * 1024
        ),
        name="projector_attention",
    )(
        *smalls,
        patches,
        w_proj,
        w_qkv,
    )
    return pl.pallas_call(
        functools.partial(place_kernel, heads, img_most),
        out_shape=jax.ShapeDtypeStruct((rows, out_cols), BF16),
        in_specs=[hbm] * 4,
        out_specs=hbm,
        scratch_shapes=[
            pltpu.VMEM(cols.shape, I32),
            pltpu.VMEM(lines.shape, I32),
            pltpu.VMEM((box_rows, prob_cols + value_cols), BF16),
            pltpu.VMEM((rows, out_cols), BF16),
            dma((4,)),
            dma((rows // TILE,)),
        ],
        name="place",
    )(cols, lines, probs, values)


def solution(mesh):
    in_specs = (
        P(("dp", "mp"), None),
        P(),
        P(),
        P(None, "mp"),
        P("mp"),
        P(),
        P(None, "mp"),
        P(),
        P(),
    )
    out_specs = P("dp", "mp")
    return jax.shard_map(local, mesh=mesh, in_specs=in_specs, out_specs=out_specs, check_vma=False)
```

time: 42.8 us -> 35.9 us (0.84)
  Pallas kernels: 42.6 us -> 35.6 us
    pallas_call x1, Pallas kernels: 39 us -> 32.6 us  [local(): pl.pallas_call(functools.partial(kernel, senders, order), out_shape=[jax....]
    pallas_call x1, Pallas kernels: 3.58 us -> 3.06 us  [local(): pl.pallas_call(functools.partial(place_kernel, heads, img_most), out_shap...]
where the time goes in v2:
time: 35.9 us; the launch traced here: 35.8 us
  Pallas kernels  35.6 us (99%)
    pallas_call x1, Pallas kernels, local(): pl.pallas_call(functools.partial(kernel, senders, order), out_shape=[jax....  32.6 us
    pallas_call x1, Pallas kernels, local(): pl.pallas_call(functools.partial(place_kernel, heads, img_most), out_shap...  3.06 us

profile of v2, /device:TPU:0, one launch (start us, length us, event | category | flops | bytes accessed | tf_op | source)
XLA Modules:
  0.0 35.8 jit_solution(1956109257156265699)
XLA Ops:
  0.0 32.6 %projector_attention.1 = (bf16[512,128]{1,0:T(8,128)(2,1)}, bf16[512,256]{1,0:T(8,128)(2,1)}, s32[512,128]{1,0:T(8,128)}, s32[8,512]{1,0:T(8,128)}) custom-call(bf16[3200]{0:T(1024)(128)(2,1)} %ln_gain_in.1, bf16[3200]{0:T(1024)(128)(2,1)} %ln_bias_in.1, bf16[2048]{0:T(1024)(128)(2,1)} %proj_bias_in.1, bf16[4096]{0:T(1024)(128)(2,1)} %rms_gain_in.1, ...), custom_call_target="tpu_custom_call" | custom-call | tf_op jit(solution)/shard_map/projector_attention/pallas_call | solution.py:581
  32.6 3.1 %place.1 = bf16[512,1024]{1,0:T(8,128)(2,1)} custom-call(s32[512,128]{1,0:T(8,128)} %get-tuple-element.9.refs_0_, s32[8,512]{1,0:T(8,128)} %get-tuple-element.10.refs_1_, bf16[512,128]{1,0:T(8,128)(2,1)} %get-tuple-element.11.refs_2_, bf16[512,256]{1,0:T(8,128)(2,1)} %get-tuple-element.12.refs_3_), custom_call_target="tpu_custom_call" | custom-call | tf_op jit(solution)/shard_map/place/pallas_call | solution.py:638

commit v3 on v2

--- a/solution.py
+++ b/solution.py
@@ -25,8 +25,12 @@
 MESH = pl.DeviceIdType.MESH
 
 
-def shift_order(senders):
-    return sorted(range(senders), key=lambda v: (abs(v - senders // 2), v))
+def exclusive_or(a, b, senders):
+    total, bit = 0, 1
+    while bit < senders:
+        total = total + lax.rem(lax.div(a, bit) + lax.div(b, bit), 2) * bit
+        bit *= 2
+    return total
 
 
 def rotary_table(positions):
@@ -58,7 +62,6 @@
 
 def kernel(
     senders,
-    order,
     ln_gain_in,
     ln_bias_in,
     proj_bias_in,
@@ -110,10 +113,8 @@
     hid_recv,
     sq_send,
     sq_recv,
-    probs_send,
-    probs_recv,
-    values_send,
-    values_recv,
+    probs_sems,
+    values_sems,
 ):
     me = lax.axis_index("dp")
     core = lax.axis_index("mp")
@@ -145,7 +146,7 @@
 
     def w1_copy(j):
         cols = pl.ds(j * COL_TILE, COL_TILE)
-        return pltpu.make_async_copy(w_proj.at[:, cols], w1.at[:, cols], w1_sem.at[j])
+        return pltpu.make_async_copy(w_proj.at[:, cols], w1.at[:, cols], w1_sem)
 
     def w2_copy(j):
         g = j // 2
@@ -155,17 +156,17 @@
         else:
             source, to, width = first + qk_group, qk_cols + g * HEAD_SIZE, HEAD_SIZE
         return pltpu.make_async_copy(
-            w_qkv.at[:, pl.ds(source, width)], w2.at[:, pl.ds(to, width)], w2_sem.at[j]
+            w_qkv.at[:, pl.ds(source, width)], w2.at[:, pl.ds(to, width)], w2_sem
         )
 
     smalls = [
         pltpu.make_async_copy(there, here, small_sem.at[i])
         for i, (there, here) in enumerate(
             [
+                (ln_gain_in, ln_gain),
+                (ln_bias_in, ln_bias),
                 (counts_in, counts),
                 (source_shift_in, source_shift),
-                (ln_gain_in, ln_gain),
-                (ln_bias_in, ln_bias),
                 (proj_bias_in, proj_bias),
                 (rms_gain_in, rms_gain),
                 (table_in, table),
@@ -178,6 +179,8 @@
         raw_copy(i).start()
     for copy in smalls[2:]:
         copy.start()
+    for j in range(tiles1 // 2):
+        w1_copy(j).start()
 
     barrier = pltpu.get_barrier_semaphore()
     pl.semaphore_signal(barrier, inc=1, device_id={"mp": peer}, device_id_type=MESH)
@@ -187,6 +190,46 @@
         )
 
     for copy in smalls[:2]:
+        copy.wait()
+    for j in range(tiles1 // 2, tiles1):
+        w1_copy(j).start()
+    gain_f = ln_gain[...].reshape(1, -1).astype(F32)
+    bias_f = ln_bias[...].reshape(1, -1).astype(F32)
+    def widen(first, values):
+        for h in range(2):
+            for b in range(blocks):
+                at = pl.ds((first + 8 * h) * blocks + b, 8, stride=blocks)
+                spread[at, :] = values[8 * h : 8 * h + 8, b * LANES : (b + 1) * LANES]
+
+    def norm_copy(i):
+        mine = normed.at[pl.ds(pl.multiple_of(core * half + i * part, part), part)]
+        return pltpu.make_async_remote_copy(
+            src_ref=mine,
+            dst_ref=mine,
+            send_sem=norm_send,
+            recv_sem=norm_recv.at[i],
+            device_id={"mp": peer},
+            device_id_type=MESH,
+        )
+
+    for i in range(parts):
+        raw_copy(i).wait()
+
+        @pl.loop(0, part // 16, unroll=4)
+        def _(r):
+            values = raw[pl.ds(pl.multiple_of(i * part + r * 16, 16), 16), :].astype(F32)
+            centred = values - jnp.mean(values, axis=-1, keepdims=True)
+            variance = jnp.mean(centred * centred, axis=-1, keepdims=True)
+            scaled = centred * lax.rsqrt(variance + norm_epsilon) * gain_f + bias_f
+            first = pl.multiple_of(core * half + i * part + r * 16, 16)
+            normed[pl.ds(first, 16), :] = scaled.astype(BF16)
+            widen(first, scaled)
+
+        if i == 0:
+            pl.semaphore_wait(barrier, senders)
+        norm_copy(i).start()
+
+    for copy in smalls[2:]:
         copy.wait()
     sq = (images, images)
     k_at, l_at = iota(sq, 0), iota(sq, 1)
@@ -213,14 +256,17 @@
     shift = to_col(shift_row)
     dest = me - shift
     dest = jnp.where(dest < 0, dest + senders, dest)
-    place = jnp.zeros((images, 1), I32)
-    for v in range(senders):
-        place = jnp.where(shift == order[v], v, place)
+    source = lax.rem(me + shift, senders)
     there = tile_at == dest * tiles_dev + own_tile
     starts = lane_sum(jnp.where(before, to_row(lane_sum(jnp.where(there, counts_by, 0))), 0))
     far_offset = lane_sum(jnp.where(there, earlier_by, 0))
     rank = lane_sum(jnp.where(before & (shift_row == shift), 1, 0))
-    slot = place * pair_slots + rank
+
+    def slot_of(partner):
+        apart = exclusive_or(jnp.broadcast_to(me, partner.shape), partner, senders)
+        return (senders - 1 - apart) * pair_slots + rank
+
+    slot = slot_of(dest)
 
     slot_hit = slot == iota((images, LANES), 1)
     plan[0:1, :] = row_sum(jnp.where(slot_hit, starts * blocks, 0))
@@ -228,50 +274,9 @@
     plan_copy = pltpu.make_async_copy(plan, plan_at, plan_sem)
     plan_copy.start()
 
-    for copy in smalls[2:]:
-        copy.wait()
-    gain_f = ln_gain[...].reshape(1, -1).astype(F32)
-    bias_f = ln_bias[...].reshape(1, -1).astype(F32)
     bias[0:1, :] = proj_bias[...].reshape(1, -1).astype(F32)
     gains = rms_gain[...].reshape(1, -1).astype(F32)
     bias[1:2, :] = jnp.where(core == 0, gains[:, :half_cols], gains[:, half_cols:])
-
-    def widen(first, values):
-        for h in range(2):
-            for b in range(blocks):
-                at = pl.ds((first + 8 * h) * blocks + b, 8, stride=blocks)
-                spread[at, :] = values[8 * h : 8 * h + 8, b * LANES : (b + 1) * LANES]
-
-    def norm_copy(i):
-        mine = normed.at[pl.ds(pl.multiple_of(core * half + i * part, part), part)]
-        return pltpu.make_async_remote_copy(
-            src_ref=mine,
-            dst_ref=mine,
-            send_sem=norm_send.at[i],
-            recv_sem=norm_recv.at[i],
-            device_id={"mp": peer},
-            device_id_type=MESH,
-        )
-
-    for i in range(parts):
-        raw_copy(i).wait()
-        if i == 0:
-            for j in range(tiles1):
-                w1_copy(j).start()
-
-        @pl.loop(0, part // 16, unroll=4)
-        def _(r):
-            values = raw[pl.ds(pl.multiple_of(i * part + r * 16, 16), 16), :].astype(F32)
-            centred = values - jnp.mean(values, axis=-1, keepdims=True)
-            variance = jnp.mean(centred * centred, axis=-1, keepdims=True)
-            scaled = centred * lax.rsqrt(variance + norm_epsilon) * gain_f + bias_f
-            first = pl.multiple_of(core * half + i * part + r * 16, 16)
-            normed[pl.ds(first, 16), :] = scaled.astype(BF16)
-            widen(first, scaled)
-
-        if i == 0:
-            pl.semaphore_wait(barrier, senders)
-        norm_copy(i).start()
 
     spread[rows * blocks :, :] = jnp.zeros((img_most * blocks, LANES), F32)
 
@@ -280,7 +285,7 @@
     my_off = lane_sum(jnp.where(here, earlier_by, 0))
     my_row = to_row(my_col)
     my_off_row = to_row(my_off)
-    slot_row = to_row(slot)
+    slot_row = to_row(slot_of(source))
     image_row, t_col = iota((TILE, images), 1), iota((TILE, images), 0)
     image_col, t_row = iota((images, TILE), 0), iota((images, TILE), 1)
     lane_at = iota((TILE, LANES), 1)
@@ -335,28 +340,30 @@
     def copy_squares(c):
         return to_peer(squares.at[core, pl.ds(c * CHUNK, CHUNK)], sq_send.at[c], sq_recv.at[c])
 
-    def exchange(o, outbox, inbox, send_sem, recv_sem):
+    far_rows = pl.ds(0, box_rows - block)
+
+    def exchange(o, outbox, inbox, sems):
         at = pl.ds(o * block, block)
         if o == senders - 1:
-            return pltpu.make_async_copy(outbox.at[at], inbox.at[at], send_sem.at[o])
+            return pltpu.make_async_copy(outbox.at[at], inbox.at[at], sems.at[2])
         return pltpu.make_async_remote_copy(
             src_ref=outbox.at[at],
             dst_ref=inbox.at[at],
-            send_sem=send_sem.at[o],
-            recv_sem=recv_sem.at[o],
-            device_id={"dp": lax.rem(me + senders - order[o], senders)},
+            send_sem=sems.at[0],
+            recv_sem=sems.at[1],
+            device_id={"dp": exclusive_or(me, senders - 1 - o, senders)},
             device_id_type=MESH,
         )
 
     def copy_probs(o):
-        return exchange(o, probs_at, box_probs, probs_send, probs_recv)
+        return exchange(o, probs_at, box_probs, probs_sems)
 
     def copy_values(o):
-        return exchange(o, values_at, box_values, values_send, values_recv)
-
-
-    @pl.loop(0, slots, unroll=2)
-    def _(i):
+        return exchange(o, values_at, box_values, values_sems)
+
+    slots_chunk = CHUNK // img_most
+
+    def pick(i):
         first = plan_at[0, i]
         to = pl.ds(pl.multiple_of(i * img_most, img_most), img_most)
         for b in range(blocks):
@@ -368,17 +375,14 @@
                 axis=0,
             ).astype(BF16)
 
-    def project(c):
+    def project(c, low, high):
         at = pl.ds(c * CHUNK, CHUNK)
-        for j in range(tiles1):
-            if c == 0 and j % 2 == 0:
-                w1_copy(j).wait()
-                w1_copy(j + 1).wait()
-                if j + 2 == tiles1:
-                    for g in range(2 * groups):
-                        w2_copy(g).start()
+        for j in range(low, high):
             cols = slice(j * COL_TILE, (j + 1) * COL_TILE)
             pre = jnp.dot(picked[at, :], w1[:, cols], preferred_element_type=F32)
+            if c == 0 and chunks > 1:
+                for i in range(slots_chunk * j // tiles1, slots_chunk * (j + 1) // tiles1):
+                    pick(slots_chunk + i)
             y = gelu(pre + bias[0:1, cols])
             z = y * y
             total = z[:, :LANES]
@@ -390,6 +394,8 @@
                 squares[core, at, :] += total
             to = pl.ds(pl.multiple_of(core * half_cols + j * COL_TILE, COL_TILE), COL_TILE)
             hidden[at, to] = (y * bias[1:2, cols]).astype(BF16)
+
+    def send(c):
         copy_squares(c).start()
         copy_hidden(c).start()
 
@@ -406,20 +412,21 @@
     def qk(c, j):
         proj[c % 2, :, qk_tiles[j]] = product(c, qk_tiles[j])
 
-    def values(c):
-        at = pl.ds(c * CHUNK, CHUNK)
+    def arrived(c):
         copy_squares(c).wait_recv()
         copy_hidden(c).wait_recv()
-        if c == 0:
-            for j in range(2 * groups):
-                w2_copy(j).wait()
+
+    def values(c, work):
+        at = pl.ds(c * CHUNK, CHUNK)
         total = lane_sum(squares[0, at, :] + squares[1, at, :])
         scale = lax.rsqrt(total * (1.0 / (2 * half_cols)) + rms_epsilon)
         value_rows = product(c, slice(qk_cols, qkv_cols))
-        qk(c, 0)
+        work()
         values_at[at, :] = (value_rows * scale).astype(BF16)
         cos_at[at, :] *= scale
         sin_at[at, :] *= scale
+
+    def send_values(c):
         for o in range(c * CHUNK // block, (c + 1) * CHUNK // block):
             copy_values(o).start()
 
@@ -448,41 +455,74 @@
             probs = weights / row_sum(weights)
             seen += [probs[:, i * TILE : (i + 1) * TILE] for i in range(QUERY_PER_KEY)]
         probs_at[to, :] = jnp.concatenate(seen, axis=0).T.astype(BF16)
+
+    def send_probs(c, first):
         for o in range((c * CHUNK + first) // block, (c * CHUNK + first + TILE) // block):
             copy_probs(o).start()
 
+
+    pl.loop(0, slots_chunk, unroll=2)(pick)
+    if chunks > 2:
+        pl.loop(2 * slots_chunk, slots, unroll=2)(pick)
+    pltpu.make_async_copy(w_proj, w1, w1_sem).wait()
+    for j in range(2 * groups):
+        w2_copy(j).start()
+    project(0, 0, tiles1)
+    send(0)
     tiles = CHUNK // TILE
-    project(0)
-    if chunks > 1:
-        project(1)
-    values(0)
-    for j in range(1, len(qk_tiles)):
-        qk(0, j)
     for c in range(chunks):
+        more = c + 1 < chunks
+        if c == 0:
+            if more:
+                project(1, 0, tiles1 - 1)
+            arrived(0)
+            pltpu.make_async_copy(w_qkv, w2, w2_sem).wait()
+            values(0, lambda: project(1, tiles1 - 1, tiles1) if more else None)
+            send_values(0)
+            if more:
+                send(1)
+            for j in range(len(qk_tiles)):
+                qk(0, j)
         if c + 2 < chunks:
-            project(c + 2)
-        if c + 1 < chunks:
-            values(c + 1)
-        for j in range(max(tiles, len(qk_tiles))):
-            if c + 1 < chunks and j + 1 < len(qk_tiles):
-                qk(c + 1, j + 1)
-            if j < tiles:
-                attend(c, j * TILE)
-
-    for copy in (copy_values, copy_probs):
-        for o in range(senders - 1):
-            copy(o).wait_recv()
-        copy(senders - 1).wait()
+            project(c + 2, 0, tiles1)
+        if more:
+            arrived(c + 1)
+            if c + 2 < chunks:
+                send(c + 2)
+
+            def beside():
+                qk(c + 1, 0)
+                for t in range(tiles):
+                    attend(c, t * TILE)
+
+            values(c + 1, beside)
+            for t in range(tiles):
+                send_probs(c, t * TILE)
+            send_values(c + 1)
+            for j in range(1, len(qk_tiles)):
+                qk(c + 1, j)
+        else:
+            for t in range(tiles):
+                attend(c, t * TILE)
+                send_probs(c, t * TILE)
+
+    for outbox, inbox, sems in (
+        (values_at, box_values, values_sems),
+        (probs_at, box_probs, probs_sems),
+    ):
+        exchange(senders - 1, outbox, inbox, sems).wait()
+        landed = inbox.at[far_rows]
+        pltpu.make_async_copy(landed, landed, sems.at[1]).wait()
     for copy in meta:
         copy.wait()
-    for i in range(parts):
-        norm_copy(i).wait_send()
+    sent = normed.at[pl.ds(pl.multiple_of(core * half, half), half)]
+    pltpu.make_async_copy(sent, sent, norm_send).wait()
     for c in range(chunks):
         copy_squares(c).wait_send()
         copy_hidden(c).wait_send()
-    for copy in (copy_values, copy_probs):
-        for o in range(senders - 1):
-            copy(o).wait_send()
+    for outbox, sems in ((values_at, values_sems), (probs_at, probs_sems)):
+        left = outbox.at[far_rows]
+        pltpu.make_async_copy(left, left, sems.at[0]).wait()
 
 
 def place_kernel(heads, img_most, *refs):
@@ -552,7 +592,6 @@
     patches, ln_gain, ln_bias, w_proj, proj_bias, rms_gain, w_qkv, image_counts, source_shift
 ):
     senders = lax.axis_size("dp")
-    order = shift_order(senders)
     half, d_vit = patches.shape
     rows = 2 * half
     parts = half // 64
@@ -579,7 +618,7 @@
         jnp.asarray(rotary_table(TILE + img_most)),
     )
     probs, values, cols, lines = pl.pallas_call(
-        functools.partial(kernel, senders, order),
+        functools.partial(kernel, senders),
         out_shape=[
             jax.ShapeDtypeStruct((box_rows, prob_cols), BF16),
             jax.ShapeDtypeStruct((box_rows, value_cols), BF16),
@@ -610,20 +649,18 @@
             pltpu.SMEM((8, LANES), I32),
             dma((len(smalls),)),
             dma((parts,)),
-            dma((half_cols // COL_TILE,)),
-            dma((2 * groups,)),
+            dma,
+            dma,
             dma,
             dma((2,)),
-            dma((parts,)),
+            dma,
             dma((parts,)),
             dma((chunks,)),
             dma((chunks,)),
             dma((chunks,)),
             dma((chunks,)),
-            dma((senders,)),
-            dma((senders,)),
-            dma((senders,)),
-            dma((senders,)),
+            dma((3,)),
+            dma((3,)),
         ],
         compiler_params=pltpu.CompilerParams(
             collective_id=0, has_side_effects=True, vmem_limit_bytes=60 * 1024 * 1024

time: 35.9 us -> 34.7 us (0.967)
  Pallas kernels: 35.6 us -> 34.3 us
    pallas_call x1, Pallas kernels: 32.6 us -> 31.3 us  [local(): pl.pallas_call(functools.partial(kernel, senders), out_shape=[jax.ShapeDt...]
where the time goes in v3:
time: 34.7 us; the launch traced here: 34.5 us
  Pallas kernels  34.3 us (99%)
    pallas_call x1, Pallas kernels, local(): pl.pallas_call(functools.partial(kernel, senders), out_shape=[jax.ShapeDt...  31.3 us
    pallas_call x1, Pallas kernels, local(): pl.pallas_call(functools.partial(place_kernel, heads, img_most), out_shap...  3.06 us

profile of v3, /device:TPU:0, one launch (start us, length us, event | category | flops | bytes accessed | tf_op | source)
XLA Modules:
  0.0 34.5 jit_solution(14569492996570322719)
XLA Ops:
  0.0 31.3 %projector_attention.1 = (bf16[512,128]{1,0:T(8,128)(2,1)}, bf16[512,256]{1,0:T(8,128)(2,1)}, s32[512,128]{1,0:T(8,128)}, s32[8,512]{1,0:T(8,128)}) custom-call(bf16[3200]{0:T(1024)(128)(2,1)} %ln_gain_in.1, bf16[3200]{0:T(1024)(128)(2,1)} %ln_bias_in.1, bf16[2048]{0:T(1024)(128)(2,1)} %proj_bias_in.1, bf16[4096]{0:T(1024)(128)(2,1)} %rms_gain_in.1, ...), custom_call_target="tpu_custom_call" | custom-call | tf_op jit(solution)/shard_map/projector_attention/pallas_call | solution.py:620
  31.3 3.1 %place.1 = bf16[512,1024]{1,0:T(8,128)(2,1)} custom-call(s32[512,128]{1,0:T(8,128)} %get-tuple-element.9.refs_0_, s32[8,512]{1,0:T(8,128)} %get-tuple-element.10.refs_1_, bf16[512,128]{1,0:T(8,128)(2,1)} %get-tuple-element.11.refs_2_, bf16[512,256]{1,0:T(8,128)(2,1)} %get-tuple-element.12.refs_3_), custom_call_target="tpu_custom_call" | custom-call | tf_op jit(solution)/shard_map/place/pallas_call | solution.py:675

commit v4 on v3

--- a/solution.py
+++ b/solution.py
@@ -173,6 +173,13 @@
             ]
         )
     ]
+    barrier = pltpu.get_barrier_semaphore()
+    pl.semaphore_signal(barrier, inc=1, device_id={"mp": peer}, device_id_type=MESH)
+    for v in range(1, senders):
+        pl.semaphore_signal(
+            barrier, inc=1, device_id={"dp": lax.rem(me + v, senders)}, device_id_type=MESH
+        )
+
     for copy in smalls[:2]:
         copy.start()
     for i in range(parts):
@@ -181,13 +188,6 @@
         copy.start()
     for j in range(tiles1 // 2):
         w1_copy(j).start()
-
-    barrier = pltpu.get_barrier_semaphore()
-    pl.semaphore_signal(barrier, inc=1, device_id={"mp": peer}, device_id_type=MESH)
-    for v in range(1, senders):
-        pl.semaphore_signal(
-            barrier, inc=1, device_id={"dp": lax.rem(me + v, senders)}, device_id_type=MESH
-        )
 
     for copy in smalls[:2]:
         copy.wait()

time: 34.7 us -> 34.7 us (level)
  no operation moved by 1% of the time
where the time goes in v4:
time: 34.7 us; the launch traced here: 34.5 us
  Pallas kernels  34.3 us (99%)
    pallas_call x1, Pallas kernels, local(): pl.pallas_call(functools.partial(kernel, senders), out_shape=[jax.ShapeDt...  31.2 us
    pallas_call x1, Pallas kernels, local(): pl.pallas_call(functools.partial(place_kernel, heads, img_most), out_shap...  3.06 us

profile of v4, /device:TPU:0, one launch (start us, length us, event | category | flops | bytes accessed | tf_op | source)
XLA Modules:
  0.0 34.5 jit_solution(2735881670819055307)
XLA Ops:
  0.0 31.2 %projector_attention.1 = (bf16[512,128]{1,0:T(8,128)(2,1)}, bf16[512,256]{1,0:T(8,128)(2,1)}, s32[512,128]{1,0:T(8,128)}, s32[8,512]{1,0:T(8,128)}) custom-call(bf16[3200]{0:T(1024)(128)(2,1)} %ln_gain_in.1, bf16[3200]{0:T(1024)(128)(2,1)} %ln_bias_in.1, bf16[2048]{0:T(1024)(128)(2,1)} %proj_bias_in.1, bf16[4096]{0:T(1024)(128)(2,1)} %rms_gain_in.1, ...), custom_call_target="tpu_custom_call" | custom-call | tf_op jit(solution)/shard_map/projector_attention/pallas_call | solution.py:620
  31.2 3.1 %place.1 = bf16[512,1024]{1,0:T(8,128)(2,1)} custom-call(s32[512,128]{1,0:T(8,128)} %get-tuple-element.9.refs_0_, s32[8,512]{1,0:T(8,128)} %get-tuple-element.10.refs_1_, bf16[512,128]{1,0:T(8,128)(2,1)} %get-tuple-element.11.refs_2_, bf16[512,256]{1,0:T(8,128)(2,1)} %get-tuple-element.12.refs_3_), custom_call_target="tpu_custom_call" | custom-call | tf_op jit(solution)/shard_map/place/pallas_call | solution.py:675
